TPU v7x, 256 devices: a whole 4x4x8 slice. The times are simulated.
256 devices in a mesh: rep: 32 (over z_lo, x, core), ep: 8 (over z_hi, y).
Axes of the slice: x: 4, y: 4, z: 8 (z_hi: 2, z_lo: 4; z = z_hi * 4 + z_lo), core: 2. Of those that a mesh axis runs over, the one named last changes fastest.
Arguments:
- tokens: bfloat16 [2, 1024, 4096], P(None, 'ep', 'rep'), may hold values from -6 to 6
- expert_ids: int32 [2, 1024, 2], P(None, 'ep'), may hold values from 0 to 7, all different within a row; in each aligned block of 128 rows (0 to 127, 128 to 255, ..., all dimensions but the last counted through in order) at most 48 rows name the same one
- router_weight: bfloat16 [4096, 8], P('rep'), may hold values from -0.09375 to 0.09375
- w_gate: bfloat16 [8, 4096, 8192], P('ep', None, 'rep'), may hold values from -0.09375 to 0.09375
- w_up: bfloat16 [8, 4096, 8192], P('ep', None, 'rep'), may hold values from -0.09375 to 0.09375
- w_down: bfloat16 [8, 8192, 4096], P('ep', 'rep'), may hold values from -0.0625 to 0.0625
- cotangent: bfloat16 [2, 1024, 4096], P(None, 'ep', 'rep'), may hold values from -6 to 6
Outputs:
- mixed: bfloat16 [2, 1024, 4096], P(None, 'ep', 'rep')
- token_grad: bfloat16 [2, 1024, 4096], P(None, 'ep', 'rep')
- gate_grad: bfloat16 [8, 4096, 8192], P('ep', None, 'rep')
- up_grad: bfloat16 [8, 4096, 8192], P('ep', None, 'rep')
- down_grad: bfloat16 [8, 8192, 4096], P('ep', 'rep')
- router_grad: float32 [4096, 8], P('rep')
Inputs may be any that keep to these rules, and one draw needn't show every extreme that they name: `expert_ids`: each row names 2 different experts. Among the 128 rows of one index of ep in one microbatch no expert is named by more than 48 rows, and in every draw some expert is named by exactly 48 of them.
All inputs are finite; a program needn't handle non-finite values.
Results may differ from a plain program's by a relative error of at most 0.025.
Values may be sent and summed in bfloat16 or wider, within the bound.
A program may use at most 128 MiB of HBM per device.

v0:
```python
import jax
import jax.numpy as jnp
from jax import lax
from jax.sharding import Mesh
from jax.sharding import PartitionSpec as P

TOP = 2
REP = ("rep_0", "rep_1", "rep_2")


def copy_for_each(array, axis):
    devices = lax.axis_size(axis)
    return lax.all_to_all(
        jnp.broadcast_to(array[None], (devices, *array.shape)), axis, 0, 0, tiled=True
    )


def taken_together(array, axis):
    everything = copy_for_each(array, axis)
    return jnp.sum(everything, axis=0)


def split_up(array, dim, devices):
    dims = array.shape
    blocks = array.reshape(*dims[:dim], devices, dims[dim] // devices, *dims[dim + 1 :])
    return jnp.moveaxis(blocks, dim, 0)


def summed_on_arrival(array, axis, dim):
    blocks = split_up(array, dim, lax.axis_size(axis))
    arrived = lax.all_to_all(blocks, axis, split_axis=0, concat_axis=0, tiled=True)
    return arrived.astype(jnp.float32).sum(axis=0)


def sum_by_axis(array, axes, dim):
    far, near = axes
    blocks = split_up(array, dim, lax.axis_size(far))
    nearer = summed_on_arrival(blocks, near, dim + 1)
    arrived = lax.all_to_all(
        nearer.astype(jnp.bfloat16), far, split_axis=0, concat_axis=0, tiled=True
    )
    return arrived.astype(jnp.float32).sum(axis=0)


def contract_first(left, right):
    return lax.dot_general(
        left, right, (((0,), (0,)), ((), ())), preferred_element_type=jnp.float32
    )


def contract_last(left, right):
    return lax.dot_general(
        left, right, (((1,), (1,)), ((), ())), preferred_element_type=jnp.float32
    )


def route(route_ids, experts, capacity, slot_count):
    hits = route_ids[:, :, None] == jnp.arange(experts, dtype=jnp.int32)[None, None, :]
    per_token = jnp.sum(hits.astype(jnp.int32), axis=1)
    before = jnp.cumsum(per_token, axis=0) - per_token
    places = jnp.sum(jnp.where(hits, before[:, None, :], 0), axis=2)
    slots = route_ids * capacity + places
    match = jnp.arange(slot_count, dtype=jnp.int32)[:, None, None] == slots[None, :, :]
    token_count = route_ids.shape[0]
    source_row = jnp.sum(
        jnp.where(match, jnp.arange(token_count, dtype=jnp.int32)[None, :, None], 0), axis=(1, 2)
    )
    filled = jnp.any(match, axis=(1, 2))
    return (hits, slots, match, source_row, filled)


def pack(rows, source_row, filled, scale):
    picked = jnp.take(rows, source_row, axis=0)
    if scale is None:
        return jnp.where(filled[:, None], picked, jnp.zeros_like(picked))
    return (picked.astype(jnp.float32) * scale[:, None]).astype(jnp.bfloat16)


def deliver(rows, source_row, filled, scale):
    moved = lax.all_to_all(
        pack(rows, source_row, filled, scale), "ep", split_axis=0, concat_axis=0, tiled=True
    )
    result = lax.all_gather(moved, REP, axis=1, tiled=True)
    return result


def collect(columns):
    return lax.all_to_all(columns, "ep", split_axis=1, concat_axis=1, tiled=True)


def shards(tokens, expert_ids, router_weight, w_gate, w_up, w_down, cotangent):
    micro_count = tokens.shape[0]
    tok_rows = tokens.shape[1]
    experts = router_weight.shape[1]
    capacity = min(tok_rows, 3 * tok_rows * TOP // (2 * experts))
    slot_count = lax.axis_size("ep") * capacity
    gate_w = w_gate[0]
    up_w = w_up[0]
    down_w = w_down[0]
    gate_acc = jnp.zeros(gate_w.shape, jnp.float32)
    up_acc = jnp.zeros(up_w.shape, jnp.float32)
    down_acc = jnp.zeros(down_w.shape, jnp.float32)
    router_acc = jnp.zeros(router_weight.shape, jnp.float32)
    router_wide = router_weight.astype(jnp.float32)
    all_logits = taken_together(
        jnp.einsum("mtc,ce->mte", tokens, router_weight, preferred_element_type=jnp.float32), REP
    )
    mixed = []
    token_grad = []
    for step in range(micro_count):
        route_ids = expert_ids[step]
        hits, slots, match, source_row, filled = route(route_ids, experts, capacity, slot_count)
        logits = all_logits[step]
        chosen = jnp.sum(jnp.where(hits, logits[:, None, :], 0.0), axis=2)
        spread = chosen[:, 0] - chosen[:, 1]
        first = jax.nn.sigmoid(spread)
        second = jax.nn.sigmoid(-spread)
        gates = jnp.stack([first, second], axis=1)
        slot_gate = jnp.sum(jnp.where(match, gates[None, :, :], 0.0), axis=(1, 2))
        expert_rows = deliver(tokens[step], source_row, filled, None)
        pre_gate = jnp.dot(expert_rows, gate_w, preferred_element_type=jnp.float32)
        pre_up = jnp.dot(expert_rows, up_w, preferred_element_type=jnp.float32)
        gate_sig = jax.nn.sigmoid(pre_gate)
        gate_act = pre_gate * gate_sig
        hidden = (gate_act * pre_up).astype(jnp.bfloat16)
        outputs = sum_by_axis(
            lax.dot_general(
                down_w, hidden, (((0,), (1,)), ((), ())), preferred_element_type=jnp.float32
            ).astype(jnp.bfloat16),
            (("rep_0", "rep_1"), "rep_2"),
            0,
        ).astype(jnp.bfloat16)
        returned = collect(outputs)
        first_out = jnp.take(returned, slots[:, 0], axis=1).astype(jnp.float32)
        second_out = jnp.take(returned, slots[:, 1], axis=1).astype(jnp.float32)
        mixed.append(
            (first[None, :] * first_out + second[None, :] * second_out).T.astype(jnp.bfloat16)
        )
        cot_cols = cotangent[step].T.astype(jnp.float32)
        partial_dots = jnp.stack(
            [jnp.sum(cot_cols * first_out, axis=0), jnp.sum(cot_cols * second_out, axis=0)]
        )
        gate_dots = taken_together(partial_dots, REP)
        delta = (gate_dots[0] - gate_dots[1]) * first * second
        logit_grad = delta[:, None] * (
            hits[:, 0].astype(jnp.float32) - hits[:, 1].astype(jnp.float32)
        )
        router_acc = router_acc + jnp.dot(
            tokens[step].astype(jnp.float32).T, logit_grad, precision=lax.Precision.HIGHEST
        )
        router_in = jnp.dot(logit_grad, router_wide.T, precision=lax.Precision.HIGHEST)
        expert_cots = deliver(cotangent[step], source_row, filled, slot_gate)
        hidden_grad = contract_last(expert_cots, down_w)
        gate_pre_grad = (
            hidden_grad * pre_up * (gate_sig * (1.0 + pre_gate * (1.0 - gate_sig)))
        ).astype(jnp.bfloat16)
        up_pre_grad = (hidden_grad * gate_act).astype(jnp.bfloat16)
        down_acc = down_acc + contract_first(hidden, expert_cots)
        gate_acc = gate_acc + contract_first(expert_rows, gate_pre_grad)
        up_acc = up_acc + contract_first(expert_rows, up_pre_grad)
        input_cols = sum_by_axis(
            (contract_last(gate_w, gate_pre_grad) + contract_last(up_w, up_pre_grad)).astype(
                jnp.bfloat16
            ),
            (("rep_0", "rep_1"), "rep_2"),
            0,
        ).astype(jnp.bfloat16)
        returned_grad = collect(input_cols)
        grad_cols = jnp.take(returned_grad, slots[:, 0], axis=1).astype(jnp.float32)
        grad_cols = grad_cols + jnp.take(returned_grad, slots[:, 1], axis=1).astype(jnp.float32)
        token_grad.append((grad_cols + router_in.T).T.astype(jnp.bfloat16))
    router_total = taken_together(router_acc, "ep")
    return (
        jnp.stack(mixed),
        jnp.stack(token_grad),
        gate_acc.astype(jnp.bfloat16)[None],
        up_acc.astype(jnp.bfloat16)[None],
        down_acc.astype(jnp.bfloat16)[None],
        router_total,
    )


def solution(mesh):
    split = Mesh(mesh.devices.reshape(4, 4, 2, mesh.shape["ep"]), ("rep_0", "rep_1", "rep_2", "ep"))
    in_specs = (
        P(None, "ep", REP),
        P(None, "ep", None),
        P(REP, None),
        P("ep", None, REP),
        P("ep", None, REP),
        P("ep", REP, None),
        P(None, "ep", REP),
    )
    out_specs = (
        P(None, "ep", REP),
        P(None, "ep", REP),
        P("ep", None, REP),
        P("ep", None, REP),
        P("ep", REP, None),
        P(REP, None),
    )
    return jax.shard_map(
        shards, mesh=split, in_specs=in_specs, out_specs=out_specs, check_vma=False
    )
```

profile of v0, /device:TPU:32, one launch (start us, length us, event | category | flops | bytes accessed | tf_op | source)
XLA Modules:
  0.0 662.5 jit_solution(15481597892796571032)
XLA Ops:
  12.3 20.5 %all_to_all.156 = bf16[8,48,128]{2,1,0:T(8,128)(2,1)} all-to-all(bf16[8,48,128]{2,1,0:T(8,128)(2,1)S(1)} %bitcast.283), channel_id=1, replica_groups=mesh['rep_0'=4,'rep_1'=4,'rep_2'=2,'ep'=8] {'ep'}, dimensions={0} | all-to-all | bytes 196608 | tf_op jit(solution)/shard_map/all_to_all | solution.py:80
  34.8 13.4 %all_to_all.157 = bf16[8,48,128]{2,1,0:T(8,128)(2,1)} all-to-all(bf16[8,48,128]{2,1,0:T(8,128)(2,1)S(1)} %bitcast.284), channel_id=1, replica_groups=mesh['rep_0'=4,'rep_1'=4,'rep_2'=2,'ep'=8] {'ep'}, dimensions={0} | all-to-all | bytes 196608 | tf_op jit(solution)/shard_map/all_to_all | solution.py:80
  48.4 47.2 %all-gather.5.cloned.1.call-done = bf16[384,4096]{1,0:T(8,128)(2,1)} async-done(((bf16[384,128]{1,0:T(8,128)(2,1)}), bf16[384,4096]{1,0:T(8,128)(2,1)}) %all-gather.5.cloned.1.call-update) | async-done | bytes 3145744 | tf_op jit(solution)/shard_map/all_gather | solution.py:83
  104.2 6.1 reshape_reshape.12
  110.3 4.0 copy.110
  114.3 5.2 all-to-all-start.2
  119.5 43.7 %all-gather.7.cloned.1.call-done = bf16[384,4096]{1,0:T(8,128)(2,1)} async-done(((bf16[384,128]{1,0:T(8,128)(2,1)}), bf16[384,4096]{1,0:T(8,128)(2,1)}) %all-gather.7.cloned.1.call-update) | async-done | bytes 3145744 | tf_op jit(solution)/shard_map/all_gather | solution.py:83
  163.2 4.3 fusion.26
  168.2 5.6 all-to-all-start
  173.9 4.3 multiply_convert_fusion.4
  178.2 4.1 reduce_sum.268
  187.9 6.1 reshape_reshape.13
  194.0 4.0 copy.109
  198.0 10.4 %all_to_all.158 = bf16[2,16,128,384]{2,1,3,0:T(8,128)(2,1)} all-to-all(bf16[2,16,128,384]{2,1,3,0:T(8,128)(2,1)} %bitcast.267), channel_id=1, replica_groups=mesh['rep_0'=4,'rep_1'=4,'rep_2'=2,'ep'=8] {'rep_2'}, dimensions={0} | all-to-all | bytes 6291456 | tf_op jit(solution)/shard_map/all_to_all | solution.py:31
  208.3 8.0 %all-to-all-start.3 = ((bf16[16,128,384]{1,2,0:T(8,128)(2,1)}), bf16[16,128,384]{1,2,0:T(8,128)(2,1)}, u32[]{:S(2)}, u32[]{:S(2)}) async-start(bf16[16,128,384]{1,2,0:T(8,128)(2,1)} %copy.78), calls=%async_computation.3 | async-start | bytes 3145728 | tf_op jit(solution)/shard_map/all_to_all | solution.py:39
  216.4 4.1 reduce_sum.275
  223.4 30.0 %all-to-all-done.3 = bf16[16,128,384]{1,2,0:T(8,128)(2,1)} async-done(((bf16[16,128,384]{1,2,0:T(8,128)(2,1)}), bf16[16,128,384]{1,2,0:T(8,128)(2,1)}, u32[]{:S(2)}, u32[]{:S(2)}) %all-to-all-start.3) | async-done | bytes 1572896 | tf_op jit(solution)/shard_map/all_to_all | solution.py:39
  253.4 5.5 all-to-all-start.7
  262.8 32.1 %all-to-all-done.7 = bf16[16,128,384]{1,2,0:T(8,128)(2,1)} async-done(((bf16[16,128,384]{1,2,0:T(8,128)(2,1)}), bf16[16,128,384]{1,2,0:T(8,128)(2,1)}, u32[]{:S(2)}, u32[]{:S(2)}) %all-to-all-start.7) | async-done | bytes 1572896 | tf_op jit(solution)/shard_map/all_to_all | solution.py:39
  294.8 7.8 %all-to-all-start.4 = ((bf16[128,8,48]{0,2,1:T(8,128)(2,1)}), bf16[128,8,48]{0,2,1:T(8,128)(2,1)S(1)}, u32[]{:S(2)}, u32[]{:S(2)}) async-start(bf16[128,8,48]{0,2,1:T(8,128)(2,1)} %bitcast.15), calls=%async_computation.4 | async-start | bytes 196608 | tf_op jit(solution)/shard_map/all_to_all | solution.py:88
  305.0 8.2 %all-to-all-done.4 = bf16[128,8,48]{0,2,1:T(8,128)(2,1)S(1)} async-done(((bf16[128,8,48]{0,2,1:T(8,128)(2,1)}), bf16[128,8,48]{0,2,1:T(8,128)(2,1)S(1)}, u32[]{:S(2)}, u32[]{:S(2)}) %all-to-all-start.4) | async-done | bytes 98336 | tf_op jit(solution)/shard_map/all_to_all | solution.py:88
  318.0 8.9 %all-to-all-done.8 = bf16[128,8,48]{0,2,1:T(8,128)(2,1)S(1)} async-done(((bf16[128,8,48]{0,2,1:T(8,128)(2,1)}), bf16[128,8,48]{0,2,1:T(8,128)(2,1)S(1)}, u32[]{:S(2)}, u32[]{:S(2)}) %all-to-all-start.8) | async-done | bytes 98336 | tf_op jit(solution)/shard_map/all_to_all | solution.py:88
  329.1 6.1 all-to-all-start.18
  335.3 6.5 all-to-all-done.18
  342.2 14.1 %all_to_all.159 = bf16[8,48,128]{2,1,0:T(8,128)(2,1)} all-to-all(bf16[8,48,128]{2,1,0:T(8,128)(2,1)S(1)} %bitcast.281), channel_id=1, replica_groups=mesh['rep_0'=4,'rep_1'=4,'rep_2'=2,'ep'=8] {'ep'}, dimensions={0} | all-to-all | bytes 196608 | tf_op jit(solution)/shard_map/all_to_all | solution.py:80
  358.5 4.3 all-to-all-start.13
  362.8 6.6 all-to-all-done.13
  369.8 14.3 %all_to_all.160 = bf16[8,48,128]{2,1,0:T(8,128)(2,1)} all-to-all(bf16[8,48,128]{2,1,0:T(8,128)(2,1)S(1)} %bitcast.282), channel_id=1, replica_groups=mesh['rep_0'=4,'rep_1'=4,'rep_2'=2,'ep'=8] {'ep'}, dimensions={0} | all-to-all | bytes 196608 | tf_op jit(solution)/shard_map/all_to_all | solution.py:80
  384.5 33.7 %all-gather.11.cloned.1.call-done = bf16[384,4096]{1,0:T(8,128)(2,1)} async-done(((bf16[384,128]{1,0:T(8,128)(2,1)}), bf16[384,4096]{1,0:T(8,128)(2,1)}) %all-gather.11.cloned.1.call-update) | async-done | bytes 3145744 | tf_op jit(solution)/shard_map/all_gather | solution.py:83
  425.8 6.1 reshape_reshape.15
  431.8 3.9 copy.107
  435.8 5.4 all-to-all-start.15
  441.2 44.8 %all-gather.9.cloned.1.call-done = bf16[384,4096]{1,0:T(8,128)(2,1)} async-done(((bf16[384,128]{1,0:T(8,128)(2,1)}), bf16[384,4096]{1,0:T(8,128)(2,1)}) %all-gather.9.cloned.1.call-update) | async-done | bytes 3145744 | tf_op jit(solution)/shard_map/all_gather | solution.py:83
  493.6 8.1 %all-to-all-start.19 = ((f32[8,128,8]{1,2,0:T(8,128)}), f32[8,128,8]{1,2,0:T(8,128)S(1)}, u32[]{:S(2)}, u32[]{:S(2)}) async-start(f32[8,128,8]{1,2,0:T(8,128)} %broadcast_in_dim.184), calls=%async_computation.19 | async-start | bytes 65536 | tf_op jit(solution)/shard_map/all_to_all | solution.py:13
  501.6 5.5 fusion.5
  512.2 6.1 reshape_reshape.14
  518.3 4.0 copy.108
  522.2 10.3 %all_to_all.161 = bf16[2,16,128,384]{2,1,3,0:T(8,128)(2,1)} all-to-all(bf16[2,16,128,384]{2,1,3,0:T(8,128)(2,1)} %bitcast.268), channel_id=1, replica_groups=mesh['rep_0'=4,'rep_1'=4,'rep_2'=2,'ep'=8] {'rep_2'}, dimensions={0} | all-to-all | bytes 6291456 | tf_op jit(solution)/shard_map/all_to_all | solution.py:31
  532.6 5.3 all-to-all-start.16
  537.8 4.1 reduce_sum.278
  544.9 29.9 %all-to-all-done.16 = bf16[16,128,384]{1,2,0:T(8,128)(2,1)S(1)} async-done(((bf16[16,128,384]{1,2,0:T(8,128)(2,1)}), bf16[16,128,384]{1,2,0:T(8,128)(2,1)S(1)}, u32[]{:S(2)}, u32[]{:S(2)}) %all-to-all-start.16) | async-done | bytes 1572896 | tf_op jit(solution)/shard_map/all_to_all | solution.py:39
  575.9 5.8 all-to-all-start.11
  596.0 21.4 %all-to-all-done.11 = bf16[16,128,384]{1,2,0:T(8,128)(2,1)S(1)} async-done(((bf16[16,128,384]{1,2,0:T(8,128)(2,1)}), bf16[16,128,384]{1,2,0:T(8,128)(2,1)S(1)}, u32[]{:S(2)}, u32[]{:S(2)}) %all-to-all-start.11) | async-done | bytes 1572896 | tf_op jit(solution)/shard_map/all_to_all | solution.py:39
  617.4 9.6 %all-to-all-start.17 = ((bf16[128,8,48]{0,2,1:T(8,128)(2,1)}), bf16[128,8,48]{0,2,1:T(8,128)(2,1)S(1)}, u32[]{:S(2)}, u32[]{:S(2)}) async-start(bf16[128,8,48]{0,2,1:T(8,128)(2,1)} %bitcast.65), calls=%async_computation.17 | async-start | bytes 196608 | tf_op jit(solution)/shard_map/all_to_all | solution.py:88
  627.0 5.1 fusion.78
  632.9 4.6 all-to-all-done.17
  637.6 5.0 all-to-all-start.12
  642.6 5.9 fusion.7
  (146 shorter events, 88.3 us)
Async XLA Ops:
  7.2 94.3 %copy-start = (bf16[1,256,4096]{2,1,0:T(8,128)(2,1)S(1)}, bf16[1,256,4096]{2,1,0:T(8,128)(2,1)}, u32[]{:S(2)}) copy-start(bf16[1,256,4096]{2,1,0:T(8,128)(2,1)} %param.16) | copy-start | bytes 6291460
  7.2 41.0 %copy-start.11 = (bf16[2,128,128]{2,1,0:T(8,128)(2,1)S(1)}, bf16[2,128,128]{2,1,0:T(8,128)(2,1)}, u32[]{:S(2)}) copy-start(bf16[2,128,128]{2,1,0:T(8,128)(2,1)} %param.11) | copy-start | bytes 196612
  7.2 41.0 %copy-start.14 = (bf16[128,8]{0,1:T(8,128)(2,1)S(1)}, bf16[128,8]{0,1:T(8,128)(2,1)}, u32[]{:S(2)}) copy-start(bf16[128,8]{0,1:T(8,128)(2,1)} %param.13) | copy-start | bytes 6148
  7.2 88.4 %all-gather.5.cloned.1.call-start = ((), (), s32[]{:S(2)}) async-start(), calls=%async_computation.20 | async-start | bytes 3244032 | tf_op jit(solution)/shard_map/all_gather | solution.py:83
  32.8 130.4 %all-gather.7.cloned.1.call-start = ((), (), s32[]{:S(2)}) async-start(), calls=%async_computation.21 | async-start | bytes 3244032 | tf_op jit(solution)/shard_map/all_gather | solution.py:83
  95.6 3.7 copy-start.3
  95.6 4.1 copy-start.7
  99.7 1.8 copy-start.15
  114.3 53.2 %all-to-all-start.2 = ((bf16[2,16,128,384]{2,1,3,0:T(8,128)(2,1)}), bf16[2,16,128,384]{2,1,3,0:T(8,128)(2,1)}, u32[]{:S(2)}, u32[]{:S(2)}) async-start(bf16[2,16,128,384]{2,1,3,0:T(8,128)(2,1)} %bitcast.266), calls=%async_computation.2 | async-start | bytes 6291456 | tf_op jit(solution)/shard_map/all_to_all | solution.py:31
  168.2 29.7 %all-to-all-start = ((f32[32,2,128,8]{2,3,1,0:T(8,128)}), f32[32,2,128,8]{2,3,1,0:T(8,128)S(1)}, u32[]{:S(2)}, u32[]{:S(2)}) async-start(f32[32,2,128,8]{2,3,1,0:T(8,128)} %broadcast_in_dim.162), calls=%async_computation | async-start | bytes 524288 | tf_op jit(solution)/shard_map/all_to_all | solution.py:13
  208.3 45.1 %all-to-all-start.3 = ((bf16[16,128,384]{1,2,0:T(8,128)(2,1)}), bf16[16,128,384]{1,2,0:T(8,128)(2,1)}, u32[]{:S(2)}, u32[]{:S(2)}) async-start(bf16[16,128,384]{1,2,0:T(8,128)(2,1)} %copy.78), calls=%async_computation.3 | async-start | bytes 3145728 | tf_op jit(solution)/shard_map/all_to_all | solution.py:39
  220.4 38.5 %copy-start.12 = (bf16[2,128,128]{2,1,0:T(8,128)(2,1)S(1)}, bf16[2,128,128]{2,1,0:T(8,128)(2,1)}, u32[]{:S(2)}) copy-start(bf16[2,128,128]{2,1,0:T(8,128)(2,1)} %param.17) | copy-start | bytes 196612
  220.4 40.0 %copy-start.13 = (s32[2,128,2]{1,2,0:T(2,128)S(1)}, s32[2,128,2]{1,2,0:T(2,128)}, u32[]{:S(2)}) copy-start(s32[2,128,2]{1,2,0:T(2,128)} %param.12) | copy-start | bytes 6148
  253.4 41.4 %all-to-all-start.7 = ((bf16[16,128,384]{1,2,0:T(8,128)(2,1)}), bf16[16,128,384]{1,2,0:T(8,128)(2,1)}, u32[]{:S(2)}, u32[]{:S(2)}) async-start(bf16[16,128,384]{1,2,0:T(8,128)(2,1)} %copy.84), calls=%async_computation.7 | async-start | bytes 3145728 | tf_op jit(solution)/shard_map/all_to_all | solution.py:39
  294.8 18.3 %all-to-all-start.4 = ((bf16[128,8,48]{0,2,1:T(8,128)(2,1)}), bf16[128,8,48]{0,2,1:T(8,128)(2,1)S(1)}, u32[]{:S(2)}, u32[]{:S(2)}) async-start(bf16[128,8,48]{0,2,1:T(8,128)(2,1)} %bitcast.15), calls=%async_computation.4 | async-start | bytes 196608 | tf_op jit(solution)/shard_map/all_to_all | solution.py:88
  313.2 13.7 %all-to-all-start.8 = ((bf16[128,8,48]{0,2,1:T(8,128)(2,1)}), bf16[128,8,48]{0,2,1:T(8,128)(2,1)S(1)}, u32[]{:S(2)}, u32[]{:S(2)}) async-start(bf16[128,8,48]{0,2,1:T(8,128)(2,1)} %bitcast.34), calls=%async_computation.8 | async-start | bytes 196608 | tf_op jit(solution)/shard_map/all_to_all | solution.py:88
  329.1 12.7 %all-to-all-start.18 = ((f32[32,2,128]{2,1,0:T(2,128)}), f32[32,2,128]{2,1,0:T(2,128)S(1)}, u32[]{:S(2)}, u32[]{:S(2)}) async-start(f32[32,2,128]{2,1,0:T(2,128)} %broadcast_in_dim.180), calls=%async_computation.18 | async-start | bytes 65536 | tf_op jit(solution)/shard_map/all_to_all | solution.py:13
  335.3 82.9 %all-gather.11.cloned.1.call-start = ((), (), s32[]{:S(2)}) async-start(), calls=%async_computation.23 | async-start | bytes 3244032 | tf_op jit(solution)/shard_map/all_gather | solution.py:83
  358.5 10.9 %all-to-all-start.13 = ((f32[32,2,128]{2,1,0:T(2,128)}), f32[32,2,128]{2,1,0:T(2,128)S(1)}, u32[]{:S(2)}, u32[]{:S(2)}) async-start(f32[32,2,128]{2,1,0:T(2,128)} %broadcast_in_dim.178), calls=%async_computation.13 | async-start | bytes 65536 | tf_op jit(solution)/shard_map/all_to_all | solution.py:13
  362.8 123.2 %all-gather.9.cloned.1.call-start = ((), (), s32[]{:S(2)}) async-start(), calls=%async_computation.22 | async-start | bytes 3244032 | tf_op jit(solution)/shard_map/all_gather | solution.py:83
  418.1 3.2 copy-start.5
  421.4 1.6 copy-start.8
  435.8 57.2 %all-to-all-start.15 = ((bf16[2,16,128,384]{2,1,3,0:T(8,128)(2,1)}), bf16[2,16,128,384]{2,1,3,0:T(8,128)(2,1)}, u32[]{:S(2)}, u32[]{:S(2)}) async-start(bf16[2,16,128,384]{2,1,3,0:T(8,128)(2,1)} %bitcast.265), calls=%async_computation.15 | async-start | bytes 6291456 | tf_op jit(solution)/shard_map/all_to_all | solution.py:31
  486.0 3.3 copy-start.6
  489.3 12.4 %copy-start.9 = (bf16[1,4096,256]{2,1,0:T(8,128)(2,1)S(1)}, bf16[1,4096,256]{2,1,0:T(8,128)(2,1)}, u32[]{:S(2)}) copy-start(bf16[1,4096,256]{2,1,0:T(8,128)(2,1)} %param.15) | copy-start | bytes 6291460
  493.6 28.6 %all-to-all-start.19 = ((f32[8,128,8]{1,2,0:T(8,128)}), f32[8,128,8]{1,2,0:T(8,128)S(1)}, u32[]{:S(2)}, u32[]{:S(2)}) async-start(f32[8,128,8]{1,2,0:T(8,128)} %broadcast_in_dim.184), calls=%async_computation.19 | async-start | bytes 65536 | tf_op jit(solution)/shard_map/all_to_all | solution.py:13
  532.6 42.2 %all-to-all-start.16 = ((bf16[16,128,384]{1,2,0:T(8,128)(2,1)}), bf16[16,128,384]{1,2,0:T(8,128)(2,1)S(1)}, u32[]{:S(2)}, u32[]{:S(2)}) async-start(bf16[16,128,384]{1,2,0:T(8,128)(2,1)} %copy.91), calls=%async_computation.16 | async-start | bytes 3145728 | tf_op jit(solution)/shard_map/all_to_all | solution.py:39
  574.8 1.1 copy-start.10
  575.9 41.5 %all-to-all-start.11 = ((bf16[16,128,384]{1,2,0:T(8,128)(2,1)}), bf16[16,128,384]{1,2,0:T(8,128)(2,1)S(1)}, u32[]{:S(2)}, u32[]{:S(2)}) async-start(bf16[16,128,384]{1,2,0:T(8,128)(2,1)} %copy.87), calls=%async_computation.11 | async-start | bytes 3145728 | tf_op jit(solution)/shard_map/all_to_all | solution.py:39
  583.3 3.3 copy-start.4
  586.6 1.9 copy-start.2
  617.4 20.1 %all-to-all-start.17 = ((bf16[128,8,48]{0,2,1:T(8,128)(2,1)}), bf16[128,8,48]{0,2,1:T(8,128)(2,1)S(1)}, u32[]{:S(2)}, u32[]{:S(2)}) async-start(bf16[128,8,48]{0,2,1:T(8,128)(2,1)} %bitcast.65), calls=%async_computation.17 | async-start | bytes 196608 | tf_op jit(solution)/shard_map/all_to_all | solution.py:88
  637.6 15.6 %all-to-all-start.12 = ((bf16[128,8,48]{0,2,1:T(8,128)(2,1)}), bf16[128,8,48]{0,2,1:T(8,128)(2,1)S(1)}, u32[]{:S(2)}, u32[]{:S(2)}) async-start(bf16[128,8,48]{0,2,1:T(8,128)(2,1)} %bitcast.47), calls=%async_computation.12 | async-start | bytes 196608 | tf_op jit(solution)/shard_map/all_to_all | solution.py:88
  642.6 13.2 %copy-start.1 = (bf16[1,256,4096]{2,1,0:T(8,128)(2,1)S(1)}, bf16[1,256,4096]{2,1,0:T(8,128)(2,1)}, u32[]{:S(2)}) copy-start(bf16[1,256,4096]{2,1,0:T(8,128)(2,1)} %param.16) | copy-start | bytes 6291460
Sparse Core Ops, SparseCore 0:
  32.9 62.6 all-gather.4
  97.4 65.8 all-gather.6
  356.5 61.5 all-gather.10
  419.8 66.1 all-gather.8
where the time goes:
time: 673 us; the launch traced here: 662 us
  waiting for transfers between devices  321 us (48%)
  starting transfers between devices  85.1 us (13%)
  blocking collectives  83 us (12%)
  local copies, waits for them, and re-layouts  69.5 us (10%)
  matrix products  60.5 us (9%)
  other arithmetic  28.9 us (4%)
  between operations  14.5 us (2%)
    all_gather x4, waiting for transfers between devices, deliver(): result = lax.all_gather(moved, REP, axis=1, tiled=True)  169 us
    all_to_all x4, waiting for transfers between devices, sum_by_axis(): lax.all_to_all(nearer.astype(jnp.bfloat16), far, split_axis=0, concat_axi...  113 us
    all_to_all x4, blocking collectives, deliver(): lax.all_to_all(pack(rows, source_row, filled, scale), 'ep', split_axis=0,...  62.3 us
    another operation x8, local copies, waits for them, and re-layouts, split_up(): array.reshape(*dims[:dim], devices, dims[dim] // devices, *dims[dim + 1:])  40.2 us
    all_to_all x4, starting transfers between devices, collect(): lax.all_to_all(columns, 'ep', split_axis=1, concat_axis=1, tiled=True)  25.7 us
    all_to_all x4, waiting for transfers between devices, collect(): lax.all_to_all(columns, 'ep', split_axis=1, concat_axis=1, tiled=True)  24.9 us
    all_to_all x4, starting transfers between devices, sum_by_axis(): lax.all_to_all(nearer.astype(jnp.bfloat16), far, split_axis=0, concat_axi...  24.6 us
    all_to_all x4, starting transfers between devices, copy_for_each(): lax.all_to_all(jnp.broadcast_to(array[None], (devices, *array.shape)), ax...  24.1 us
  transfers between devices with their start and end apart: 18, of which 14 were waited for; matrix products, arithmetic and copies ran while one was open for 22% of the time, Pallas kernels for 0%

commit v1 on v0

--- a/solution.py
+++ b/solution.py
@@ -85,7 +85,15 @@
 
 
 def collect(columns):
-    return lax.all_to_all(columns, "ep", split_axis=1, concat_axis=1, tiled=True)
+
+    def wrap_yards_in(t0, net_axis):
+        mat_out = jax.lax.axis_size(net_axis)
+        vec_out = jnp.split(t0, mat_out, 1)
+        high = jnp.stack(vec_out)
+        front = jax.lax.all_to_all(high, net_axis, 0, 0)
+        return jnp.concatenate(front, 1)
+
+    return wrap_yards_in(columns, "ep")
 
 
 def shards(tokens, expert_ids, router_weight, w_gate, w_up, w_down, cotangent):

time: 673 us -> 675 us (level)
  local copies, waits for them, and re-layouts: 69.5 us -> 87.9 us
  waiting for transfers between devices: 321 us -> 304 us
    unnamed x32 -> x62, local copies, waits for them, and re-layouts: 2.77 us -> 18.6 us
    all_to_all x4, waiting for transfers between devices: 113 us -> 101 us  [sum_by_axis(): lax.all_to_all(nearer.astype(jnp.bfloat16), far, split_axis=0, concat_axi...]
  transfers between devices with their start and end apart: 18 -> 18, of which waited for: 14 -> 14; matrix products, arithmetic and copies ran while one was open for 22% -> 24% of each run, Pallas kernels for 0% -> 0%
where the time goes in v1:
time: 675 us; the launch traced here: 664 us
  waiting for transfers between devices  304 us (45%)
  local copies, waits for them, and re-layouts  87.9 us (13%)
  starting transfers between devices  87.3 us (13%)
  blocking collectives  83 us (12%)
  matrix products  60.6 us (9%)
  other arithmetic  26.3 us (4%)
  between operations  14.5 us (2%)
    all_gather x4, waiting for transfers between devices, deliver(): result = lax.all_gather(moved, REP, axis=1, tiled=True)  170 us
    all_to_all x4, waiting for transfers between devices, sum_by_axis(): lax.all_to_all(nearer.astype(jnp.bfloat16), far, split_axis=0, concat_axi...  101 us
    all_to_all x4, blocking collectives, deliver(): lax.all_to_all(pack(rows, source_row, filled, scale), 'ep', split_axis=0,...  62.4 us
    another operation x8, local copies, waits for them, and re-layouts, split_up(): array.reshape(*dims[:dim], devices, dims[dim] // devices, *dims[dim + 1:])  40.3 us
    all_to_all x4, starting transfers between devices, wrap_yards_in(): front = jax.lax.all_to_all(high, net_axis, 0, 0)  28.3 us
    all_to_all x4, starting transfers between devices, sum_by_axis(): lax.all_to_all(nearer.astype(jnp.bfloat16), far, split_axis=0, concat_axi...  24.7 us
    all_to_all x4, starting transfers between devices, copy_for_each(): lax.all_to_all(jnp.broadcast_to(array[None], (devices, *array.shape)), ax...  23.6 us
    dot_general x6, matrix products, contract_first(): lax.dot_general(left, right, (((0,), (0,)), ((), ())), preferred_element_...  21 us
  transfers between devices with their start and end apart: 18, of which 14 were waited for; matrix products, arithmetic and copies ran while one was open for 24% of the time, Pallas kernels for 0%

profile of v1, /device:TPU:32, one launch (start us, length us, event | category | flops | bytes accessed | tf_op | source)
XLA Modules:
  0.0 663.9 jit_solution(9850137715980807405)
XLA Ops:
  12.3 20.5 %all_to_all.128 = bf16[8,48,128]{2,1,0:T(8,128)(2,1)} all-to-all(bf16[8,48,128]{2,1,0:T(8,128)(2,1)S(1)} %bitcast.415), channel_id=1, replica_groups=mesh['rep_0'=4,'rep_1'=4,'rep_2'=2,'ep'=8] {'ep'}, dimensions={0} | all-to-all | bytes 196608 | tf_op jit(solution)/shard_map/all_to_all | solution.py:80
  34.8 13.4 %all_to_all.129 = bf16[8,48,128]{2,1,0:T(8,128)(2,1)} all-to-all(bf16[8,48,128]{2,1,0:T(8,128)(2,1)S(1)} %bitcast.416), channel_id=1, replica_groups=mesh['rep_0'=4,'rep_1'=4,'rep_2'=2,'ep'=8] {'ep'}, dimensions={0} | all-to-all | bytes 196608 | tf_op jit(solution)/shard_map/all_to_all | solution.py:80
  48.4 47.2 %all-gather.5.cloned.1.call-done = bf16[384,4096]{1,0:T(8,128)(2,1)} async-done(((bf16[384,128]{1,0:T(8,128)(2,1)}), bf16[384,4096]{1,0:T(8,128)(2,1)}) %all-gather.5.cloned.1.call-update) | async-done | bytes 3145744 | tf_op jit(solution)/shard_map/all_gather | solution.py:83
  104.1 6.2 reshape_reshape.12
  110.2 3.9 copy.110
  114.1 5.2 all-to-all-start.2
  119.4 43.9 %all-gather.7.cloned.1.call-done = bf16[384,4096]{1,0:T(8,128)(2,1)} async-done(((bf16[384,128]{1,0:T(8,128)(2,1)}), bf16[384,4096]{1,0:T(8,128)(2,1)}) %all-gather.7.cloned.1.call-update) | async-done | bytes 3145744 | tf_op jit(solution)/shard_map/all_gather | solution.py:83
  163.2 4.3 fusion.26
  168.2 5.6 all-to-all-start
  173.9 4.3 multiply_convert_fusion.4
  178.2 4.1 reduce_sum.268
  187.9 6.2 reshape_reshape.13
  194.1 4.0 copy.109
  198.1 10.3 %all_to_all.130 = bf16[2,16,128,384]{2,1,3,0:T(8,128)(2,1)} all-to-all(bf16[2,16,128,384]{2,1,3,0:T(8,128)(2,1)} %bitcast.399), channel_id=1, replica_groups=mesh['rep_0'=4,'rep_1'=4,'rep_2'=2,'ep'=8] {'rep_2'}, dimensions={0} | all-to-all | bytes 6291456 | tf_op jit(solution)/shard_map/all_to_all | solution.py:31
  208.4 8.0 %all-to-all-start.3 = ((bf16[16,128,384]{1,2,0:T(8,128)(2,1)}), bf16[16,128,384]{1,2,0:T(8,128)(2,1)}, u32[]{:S(2)}, u32[]{:S(2)}) async-start(bf16[16,128,384]{1,2,0:T(8,128)(2,1)} %copy.78), calls=%async_computation.3 | async-start | bytes 3145728 | tf_op jit(solution)/shard_map/all_to_all | solution.py:39
  216.5 4.1 reduce_sum.275
  223.5 30.0 %all-to-all-done.3 = bf16[16,128,384]{1,2,0:T(8,128)(2,1)} async-done(((bf16[16,128,384]{1,2,0:T(8,128)(2,1)}), bf16[16,128,384]{1,2,0:T(8,128)(2,1)}, u32[]{:S(2)}, u32[]{:S(2)}) %all-to-all-start.3) | async-done | bytes 1572896 | tf_op jit(solution)/shard_map/all_to_all | solution.py:39
  253.5 5.5 all-to-all-start.7
  267.1 27.8 %all-to-all-done.7 = bf16[16,128,384]{1,2,0:T(8,128)(2,1)} async-done(((bf16[16,128,384]{1,2,0:T(8,128)(2,1)}), bf16[16,128,384]{1,2,0:T(8,128)(2,1)}, u32[]{:S(2)}, u32[]{:S(2)}) %all-to-all-start.7) | async-done | bytes 1572896 | tf_op jit(solution)/shard_map/all_to_all | solution.py:39
  294.9 7.8 %all-to-all-start.4 = ((bf16[8,128,48]{1,2,0:T(8,128)(2,1)}), bf16[8,128,48]{1,2,0:T(8,128)(2,1)S(1)}, u32[]{:S(2)}, u32[]{:S(2)}) async-start(bf16[8,128,48]{1,2,0:T(8,128)(2,1)} %constant_dynamic-update-slice_fusion), calls=%async_computation.4 | async-start | bytes 196608 | tf_op jit(solution)/shard_map/all_to_all | solution.py:93
  309.2 4.1 all-to-all-done.4
  313.3 5.5 all-to-all-start.8
  320.2 9.1 %all-to-all-done.8 = bf16[8,128,48]{1,2,0:T(8,128)(2,1)S(1)} async-done(((bf16[8,128,48]{1,2,0:T(8,128)(2,1)}), bf16[8,128,48]{1,2,0:T(8,128)(2,1)S(1)}, u32[]{:S(2)}, u32[]{:S(2)}) %all-to-all-start.8) | async-done | bytes 98336 | tf_op jit(solution)/shard_map/all_to_all | solution.py:93
  331.6 5.6 all-to-all-start.18
  337.3 6.5 all-to-all-done.18
  344.3 14.1 %all_to_all.131 = bf16[8,48,128]{2,1,0:T(8,128)(2,1)} all-to-all(bf16[8,48,128]{2,1,0:T(8,128)(2,1)S(1)} %bitcast.413), channel_id=1, replica_groups=mesh['rep_0'=4,'rep_1'=4,'rep_2'=2,'ep'=8] {'ep'}, dimensions={0} | all-to-all | bytes 196608 | tf_op jit(solution)/shard_map/all_to_all | solution.py:80
  360.5 4.3 all-to-all-start.13
  364.9 6.6 all-to-all-done.13
  371.9 14.4 %all_to_all.132 = bf16[8,48,128]{2,1,0:T(8,128)(2,1)} all-to-all(bf16[8,48,128]{2,1,0:T(8,128)(2,1)S(1)} %bitcast.414), channel_id=1, replica_groups=mesh['rep_0'=4,'rep_1'=4,'rep_2'=2,'ep'=8] {'ep'}, dimensions={0} | all-to-all | bytes 196608 | tf_op jit(solution)/shard_map/all_to_all | solution.py:80
  386.5 33.7 %all-gather.11.cloned.1.call-done = bf16[384,4096]{1,0:T(8,128)(2,1)} async-done(((bf16[384,128]{1,0:T(8,128)(2,1)}), bf16[384,4096]{1,0:T(8,128)(2,1)}) %all-gather.11.cloned.1.call-update) | async-done | bytes 3145744 | tf_op jit(solution)/shard_map/all_gather | solution.py:83
  427.8 6.1 reshape_reshape.15
  433.8 3.9 copy.107
  437.8 5.4 all-to-all-start.15
  443.2 44.9 %all-gather.9.cloned.1.call-done = bf16[384,4096]{1,0:T(8,128)(2,1)} async-done(((bf16[384,128]{1,0:T(8,128)(2,1)}), bf16[384,4096]{1,0:T(8,128)(2,1)}) %all-gather.9.cloned.1.call-update) | async-done | bytes 3145744 | tf_op jit(solution)/shard_map/all_gather | solution.py:83
  495.6 8.1 %all-to-all-start.19 = ((f32[8,128,8]{1,2,0:T(8,128)}), f32[8,128,8]{1,2,0:T(8,128)S(1)}, u32[]{:S(2)}, u32[]{:S(2)}) async-start(f32[8,128,8]{1,2,0:T(8,128)} %broadcast_in_dim.184), calls=%async_computation.19 | async-start | bytes 65536 | tf_op jit(solution)/shard_map/all_to_all | solution.py:13
  503.7 5.4 fusion.5
  514.2 6.1 reshape_reshape.14
  520.3 4.0 copy.108
  524.3 10.4 %all_to_all.133 = bf16[2,16,128,384]{2,1,3,0:T(8,128)(2,1)} all-to-all(bf16[2,16,128,384]{2,1,3,0:T(8,128)(2,1)} %bitcast.400), channel_id=1, replica_groups=mesh['rep_0'=4,'rep_1'=4,'rep_2'=2,'ep'=8] {'rep_2'}, dimensions={0} | all-to-all | bytes 6291456 | tf_op jit(solution)/shard_map/all_to_all | solution.py:31
  534.6 5.3 all-to-all-start.16
  541.4 4.1 reduce_sum.278
  555.2 21.7 %all-to-all-done.16 = bf16[16,128,384]{1,2,0:T(8,128)(2,1)S(1)} async-done(((bf16[16,128,384]{1,2,0:T(8,128)(2,1)}), bf16[16,128,384]{1,2,0:T(8,128)(2,1)S(1)}, u32[]{:S(2)}, u32[]{:S(2)}) %all-to-all-start.16) | async-done | bytes 1572896 | tf_op jit(solution)/shard_map/all_to_all | solution.py:39
  576.8 5.9 all-to-all-start.11
  597.1 21.4 %all-to-all-done.11 = bf16[16,128,384]{1,2,0:T(8,128)(2,1)} async-done(((bf16[16,128,384]{1,2,0:T(8,128)(2,1)}), bf16[16,128,384]{1,2,0:T(8,128)(2,1)}, u32[]{:S(2)}, u32[]{:S(2)}) %all-to-all-start.11) | async-done | bytes 1572896 | tf_op jit(solution)/shard_map/all_to_all | solution.py:39
  618.4 9.6 %all-to-all-start.17 = ((bf16[8,128,48]{1,2,0:T(8,128)(2,1)}), bf16[8,128,48]{1,2,0:T(8,128)(2,1)S(1)}, u32[]{:S(2)}, u32[]{:S(2)}) async-start(bf16[8,128,48]{1,2,0:T(8,128)(2,1)} %constant_dynamic-update-slice_fusion.24), calls=%async_computation.17 | async-start | bytes 196608 | tf_op jit(solution)/shard_map/all_to_all | solution.py:93
  634.4 4.1 all-to-all-done.17
  638.6 5.5 all-to-all-start.12
  644.0 5.9 fusion.7
  (180 shorter events, 105.9 us)
Async XLA Ops:
  7.2 94.3 %copy-start = (bf16[1,256,4096]{2,1,0:T(8,128)(2,1)S(1)}, bf16[1,256,4096]{2,1,0:T(8,128)(2,1)}, u32[]{:S(2)}) copy-start(bf16[1,256,4096]{2,1,0:T(8,128)(2,1)} %param.16) | copy-start | bytes 6291460
  7.2 41.0 %copy-start.12 = (bf16[2,128,128]{2,1,0:T(8,128)(2,1)S(1)}, bf16[2,128,128]{2,1,0:T(8,128)(2,1)}, u32[]{:S(2)}) copy-start(bf16[2,128,128]{2,1,0:T(8,128)(2,1)} %param.11) | copy-start | bytes 196612
  7.2 41.0 %copy-start.15 = (bf16[128,8]{0,1:T(8,128)(2,1)S(1)}, bf16[128,8]{0,1:T(8,128)(2,1)}, u32[]{:S(2)}) copy-start(bf16[128,8]{0,1:T(8,128)(2,1)} %param.13) | copy-start | bytes 6148
  7.2 88.4 %all-gather.5.cloned.1.call-start = ((), (), s32[]{:S(2)}) async-start(), calls=%async_computation.20 | async-start | bytes 3244032 | tf_op jit(solution)/shard_map/all_gather | solution.py:83
  32.8 130.5 %all-gather.7.cloned.1.call-start = ((), (), s32[]{:S(2)}) async-start(), calls=%async_computation.21 | async-start | bytes 3244032 | tf_op jit(solution)/shard_map/all_gather | solution.py:83
  95.6 3.7 copy-start.4
  95.6 4.1 copy-start.8
  99.7 1.7 copy-start.16
  114.1 53.4 %all-to-all-start.2 = ((bf16[2,16,128,384]{2,1,3,0:T(8,128)(2,1)}), bf16[2,16,128,384]{2,1,3,0:T(8,128)(2,1)}, u32[]{:S(2)}, u32[]{:S(2)}) async-start(bf16[2,16,128,384]{2,1,3,0:T(8,128)(2,1)} %bitcast.398), calls=%async_computation.2 | async-start | bytes 6291456 | tf_op jit(solution)/shard_map/all_to_all | solution.py:31
  168.2 29.8 %all-to-all-start = ((f32[32,2,128,8]{2,3,1,0:T(8,128)}), f32[32,2,128,8]{2,3,1,0:T(8,128)S(1)}, u32[]{:S(2)}, u32[]{:S(2)}) async-start(f32[32,2,128,8]{2,3,1,0:T(8,128)} %broadcast_in_dim.162), calls=%async_computation | async-start | bytes 524288 | tf_op jit(solution)/shard_map/all_to_all | solution.py:13
  208.4 45.1 %all-to-all-start.3 = ((bf16[16,128,384]{1,2,0:T(8,128)(2,1)}), bf16[16,128,384]{1,2,0:T(8,128)(2,1)}, u32[]{:S(2)}, u32[]{:S(2)}) async-start(bf16[16,128,384]{1,2,0:T(8,128)(2,1)} %copy.78), calls=%async_computation.3 | async-start | bytes 3145728 | tf_op jit(solution)/shard_map/all_to_all | solution.py:39
  220.5 38.5 %copy-start.13 = (bf16[2,128,128]{2,1,0:T(8,128)(2,1)S(1)}, bf16[2,128,128]{2,1,0:T(8,128)(2,1)}, u32[]{:S(2)}) copy-start(bf16[2,128,128]{2,1,0:T(8,128)(2,1)} %param.17) | copy-start | bytes 196612
  220.5 40.0 %copy-start.14 = (s32[2,128,2]{1,2,0:T(2,128)S(1)}, s32[2,128,2]{1,2,0:T(2,128)}, u32[]{:S(2)}) copy-start(s32[2,128,2]{1,2,0:T(2,128)} %param.12) | copy-start | bytes 6148
  253.5 41.4 %all-to-all-start.7 = ((bf16[16,128,384]{1,2,0:T(8,128)(2,1)}), bf16[16,128,384]{1,2,0:T(8,128)(2,1)}, u32[]{:S(2)}, u32[]{:S(2)}) async-start(bf16[16,128,384]{1,2,0:T(8,128)(2,1)} %copy.84), calls=%async_computation.7 | async-start | bytes 3145728 | tf_op jit(solution)/shard_map/all_to_all | solution.py:39
  294.9 18.3 %all-to-all-start.4 = ((bf16[8,128,48]{1,2,0:T(8,128)(2,1)}), bf16[8,128,48]{1,2,0:T(8,128)(2,1)S(1)}, u32[]{:S(2)}, u32[]{:S(2)}) async-start(bf16[8,128,48]{1,2,0:T(8,128)(2,1)} %constant_dynamic-update-slice_fusion), calls=%async_computation.4 | async-start | bytes 196608 | tf_op jit(solution)/shard_map/all_to_all | solution.py:93
  313.3 16.1 %all-to-all-start.8 = ((bf16[8,128,48]{1,2,0:T(8,128)(2,1)}), bf16[8,128,48]{1,2,0:T(8,128)(2,1)S(1)}, u32[]{:S(2)}, u32[]{:S(2)}) async-start(bf16[8,128,48]{1,2,0:T(8,128)(2,1)} %constant_dynamic-update-slice_fusion.8), calls=%async_computation.8 | async-start | bytes 196608 | tf_op jit(solution)/shard_map/all_to_all | solution.py:93
  331.6 12.2 %all-to-all-start.18 = ((f32[32,2,128]{2,1,0:T(2,128)}), f32[32,2,128]{2,1,0:T(2,128)S(1)}, u32[]{:S(2)}, u32[]{:S(2)}) async-start(f32[32,2,128]{2,1,0:T(2,128)} %broadcast_in_dim.180), calls=%async_computation.18 | async-start | bytes 65536 | tf_op jit(solution)/shard_map/all_to_all | solution.py:13
  337.3 82.9 %all-gather.11.cloned.1.call-start = ((), (), s32[]{:S(2)}) async-start(), calls=%async_computation.23 | async-start | bytes 3244032 | tf_op jit(solution)/shard_map/all_gather | solution.py:83
  360.5 10.9 %all-to-all-start.13 = ((f32[32,2,128]{2,1,0:T(2,128)}), f32[32,2,128]{2,1,0:T(2,128)S(1)}, u32[]{:S(2)}, u32[]{:S(2)}) async-start(f32[32,2,128]{2,1,0:T(2,128)} %broadcast_in_dim.178), calls=%async_computation.13 | async-start | bytes 65536 | tf_op jit(solution)/shard_map/all_to_all | solution.py:13
  364.8 123.2 %all-gather.9.cloned.1.call-start = ((), (), s32[]{:S(2)}) async-start(), calls=%async_computation.22 | async-start | bytes 3244032 | tf_op jit(solution)/shard_map/all_gather | solution.py:83
  420.2 3.3 copy-start.6
  423.4 1.6 copy-start.9
  437.8 57.2 %all-to-all-start.15 = ((bf16[2,16,128,384]{2,1,3,0:T(8,128)(2,1)}), bf16[2,16,128,384]{2,1,3,0:T(8,128)(2,1)}, u32[]{:S(2)}, u32[]{:S(2)}) async-start(bf16[2,16,128,384]{2,1,3,0:T(8,128)(2,1)} %bitcast.397), calls=%async_computation.15 | async-start | bytes 6291456 | tf_op jit(solution)/shard_map/all_to_all | solution.py:31
  488.0 3.2 copy-start.7
  491.3 12.4 %copy-start.10 = (bf16[1,4096,256]{2,1,0:T(8,128)(2,1)S(1)}, bf16[1,4096,256]{2,1,0:T(8,128)(2,1)}, u32[]{:S(2)}) copy-start(bf16[1,4096,256]{2,1,0:T(8,128)(2,1)} %param.15) | copy-start | bytes 6291460
  495.6 28.7 %all-to-all-start.19 = ((f32[8,128,8]{1,2,0:T(8,128)}), f32[8,128,8]{1,2,0:T(8,128)S(1)}, u32[]{:S(2)}, u32[]{:S(2)}) async-start(f32[8,128,8]{1,2,0:T(8,128)} %broadcast_in_dim.184), calls=%async_computation.19 | async-start | bytes 65536 | tf_op jit(solution)/shard_map/all_to_all | solution.py:13
  534.6 42.2 %all-to-all-start.16 = ((bf16[16,128,384]{1,2,0:T(8,128)(2,1)}), bf16[16,128,384]{1,2,0:T(8,128)(2,1)S(1)}, u32[]{:S(2)}, u32[]{:S(2)}) async-start(bf16[16,128,384]{1,2,0:T(8,128)(2,1)} %copy.91), calls=%async_computation.16 | async-start | bytes 3145728 | tf_op jit(solution)/shard_map/all_to_all | solution.py:39
  545.5 3.1 copy-start.11
  548.6 3.4 copy-start.5
  576.8 41.6 %all-to-all-start.11 = ((bf16[16,128,384]{1,2,0:T(8,128)(2,1)}), bf16[16,128,384]{1,2,0:T(8,128)(2,1)}, u32[]{:S(2)}, u32[]{:S(2)}) async-start(bf16[16,128,384]{1,2,0:T(8,128)(2,1)} %copy.87), calls=%async_computation.11 | async-start | bytes 3145728 | tf_op jit(solution)/shard_map/all_to_all | solution.py:39
  582.7 3.4 copy-start.2
  582.7 4.1 copy-start.3
  618.4 20.1 %all-to-all-start.17 = ((bf16[8,128,48]{1,2,0:T(8,128)(2,1)}), bf16[8,128,48]{1,2,0:T(8,128)(2,1)S(1)}, u32[]{:S(2)}, u32[]{:S(2)}) async-start(bf16[8,128,48]{1,2,0:T(8,128)(2,1)} %constant_dynamic-update-slice_fusion.24), calls=%async_computation.17 | async-start | bytes 196608 | tf_op jit(solution)/shard_map/all_to_all | solution.py:93
  638.6 16.0 %all-to-all-start.12 = ((bf16[8,128,48]{1,2,0:T(8,128)(2,1)}), bf16[8,128,48]{1,2,0:T(8,128)(2,1)S(1)}, u32[]{:S(2)}, u32[]{:S(2)}) async-start(bf16[8,128,48]{1,2,0:T(8,128)(2,1)} %constant_dynamic-update-slice_fusion.16), calls=%async_computation.12 | async-start | bytes 196608 | tf_op jit(solution)/shard_map/all_to_all | solution.py:93
  644.0 13.2 %copy-start.1 = (bf16[1,256,4096]{2,1,0:T(8,128)(2,1)S(1)}, bf16[1,256,4096]{2,1,0:T(8,128)(2,1)}, u32[]{:S(2)}) copy-start(bf16[1,256,4096]{2,1,0:T(8,128)(2,1)} %param.16) | copy-start | bytes 6291460
Sparse Core Ops, SparseCore 0:
  32.9 62.6 all-gather.4
  97.4 65.8 all-gather.6
  358.5 61.5 all-gather.10
  421.8 66.1 all-gather.8
